TPU v7x, 256 devices: a whole 4x4x8 slice. The times are simulated.
256 devices in a mesh: seq: 32 (over y, x, core), head: 8 (over z).
Axes of the slice: x: 4, y: 4, z: 8, core: 2. Of those that a mesh axis runs over, the one named last changes fastest.
Arguments:
- tokens: bfloat16 [512, 4096], P('seq'), may hold values from -6 to 6
- norm_gain: bfloat16 [4096], replicated, may hold values from 0.25 to 1.75
- w_query: bfloat16 [4096, 4096], P(None, 'head'), may hold values from -0.09375 to 0.09375
- key_projection: bfloat16 [4096, 1024], P(None, 'head'), may hold values from -0.25 to 0.25
- value_projection: bfloat16 [4096, 1024], P(None, 'head'), may hold values from -0.09375 to 0.09375
- w_out: bfloat16 [4096, 4096], P('head'), may hold values from -0.09375 to 0.09375
- cache_keys: bfloat16 [8, 65536, 1024], P(None, 'seq', 'head'), may hold values from -60 to 60
- paged_value_cache: bfloat16 [8, 65536, 1024], P(None, 'seq', 'head'), may hold values from -6 to 6
- lengths: int32 [8], replicated, may hold values from 8192 to 65536
- parents: int32 [8, 64], replicated, may hold values from -1 to 62, as said below
- slot_block: int32 [8, 512], P(None, 'seq'), may hold values from 0 to 511, each once within a row
Outputs:
- mixed: bfloat16 [512, 4096], P('seq', 'head')
Inputs may be any that keep to these rules, and one draw needn't show every extreme that they name: parents[r, 0] = -1 for the root; for j >= 1, 0 <= parents[r, j] < j; the last token's parent is always token 62. Each row of slot_block is a permutation of 0 to 511.
All inputs are finite; a program needn't handle non-finite values.
Results may differ from a plain program's by a relative error of at most 0.0054.
The roundings to bfloat16 on the way count: a program that leaves them out, or rounds other values in their place, can miss the bound.
Values may be sent and summed in bfloat16 or wider, within the bound.
A program may use at most 128 MiB of HBM per device.

v0:
```python
import jax
import jax.numpy as jnp
from jax import lax
from jax.sharding import PartitionSpec as P

MODEL_WIDTH = 4096
HEAD_WIDTH = 128
TQ = 64
BLK = 128


norm_epsilon = 1e-05
masked_score = -1e30


def laid_out(blocks, dim):
    lengths = list(blocks.shape[1:])
    lengths[dim] *= blocks.shape[0]
    return jnp.moveaxis(blocks, 0, dim).reshape(lengths)


def sent_to_all(array, axis):
    size = lax.axis_size(axis)
    return lax.all_to_all(
        jnp.broadcast_to(array[None], (size, *array.shape)), axis, 0, 0, tiled=True
    )


def collect(array, axis, dim):
    return laid_out(sent_to_all(array, axis), dim)


def side_by_side(arrays, axis, dim, along):
    ends, at = ([], 0)
    for a in arrays[:-1]:
        at += a.shape[along]
        ends.append(at)
    both = jnp.concatenate(arrays, axis=along)
    return tuple(jnp.split(collect(both, axis, dim), ends, axis=along))


def in_blocks(array, dim, size):
    lengths = array.shape
    blocks = array.reshape(*lengths[:dim], size, lengths[dim] // size, *lengths[dim + 1 :])
    return jnp.moveaxis(blocks, dim, 0)


def sent_and_summed(array, axis, dim):
    blocks = in_blocks(array, dim, lax.axis_size(axis))
    arrived = lax.all_to_all(blocks, axis, split_axis=0, concat_axis=0, tiled=True)
    return arrived.astype(jnp.float32).sum(axis=0)


def ancestors(parents):
    width_tree = parents.shape[-1]
    node_ids = jnp.arange(width_tree, dtype=jnp.int32)
    reached = (parents[..., :, None] == node_ids).astype(jnp.float32)
    reached = reached + (node_ids[:, None] == node_ids[None, :]).astype(jnp.float32)
    for repeat_step in range(max(1, (width_tree - 1).bit_length())):
        reached = jnp.minimum(
            jnp.einsum("rij,rjk->rik", reached, reached, precision=lax.Precision.HIGHEST), 1.0
        )
    return reached


def finish_group(group_max, group_total, group_sum):
    floored = jnp.maximum(group_total, 1.0)
    output = (group_sum / floored[..., None]).astype(jnp.bfloat16)
    return (output, group_max + jnp.log(floored))


def per_device(
    tokens,
    norm_gain,
    w_query,
    key_projection,
    value_projection,
    w_out,
    cache_keys,
    paged_value_cache,
    lengths,
    parents,
    slot_block,
):
    inputs = tokens.astype(jnp.float32)
    normed = (
        inputs
        * lax.rsqrt(jnp.mean(inputs * inputs, axis=-1, keepdims=True) + norm_epsilon)
        * norm_gain.astype(jnp.float32)
    ).astype(jnp.bfloat16)
    queries = jnp.dot(normed, w_query, preferred_element_type=jnp.float32).astype(jnp.bfloat16)
    key_new = jnp.dot(normed, key_projection, preferred_element_type=jnp.float32).astype(
        jnp.bfloat16
    )
    value_new = jnp.dot(normed, value_projection, preferred_element_type=jnp.float32).astype(
        jnp.bfloat16
    )
    local_rows = tokens.shape[0]
    kv_heads = key_projection.shape[1] // HEAD_WIDTH
    groups = w_query.shape[1] // key_projection.shape[1]
    local_context = cache_keys.shape[1]
    requests = lengths.shape[0]
    all_rows = requests * TQ
    score_scale = HEAD_WIDTH ** (-0.5)
    row_start = lax.axis_index("seq") * local_rows
    all_queries, all_keys, all_values = side_by_side((queries, key_new, value_new), "seq", 0, 1)
    block_offsets = jnp.arange(BLK, dtype=jnp.int32)
    positions = (slot_block[:, :, None] * BLK + block_offsets[None, None, :]).reshape(
        requests, local_context
    )
    visible = (positions < lengths[:, None])[:, None, None, None, :]
    query_blocks = all_queries.reshape(requests, TQ, kv_heads, groups, HEAD_WIDTH)
    key_blocks = cache_keys.reshape(requests, local_context, kv_heads, HEAD_WIDTH)
    value_blocks = paged_value_cache.reshape(requests, local_context, kv_heads, HEAD_WIDTH)
    cache_scores = (
        jnp.einsum(
            "rthgd,rchd->rthgc", query_blocks, key_blocks, preferred_element_type=jnp.float32
        )
        * score_scale
    )
    cache_scores = jnp.where(visible, cache_scores, masked_score)
    cache_max = cache_scores.max(-1)
    cache_weights = jnp.where(visible, jnp.exp(cache_scores - cache_max[..., None]), 0.0)
    cache_total = cache_weights.sum(-1).reshape(all_rows, kv_heads, groups)
    cache_sum = jnp.einsum(
        "rthgc,rchd->rthgd",
        cache_weights.astype(jnp.bfloat16),
        value_blocks,
        preferred_element_type=jnp.float32,
    )
    cache_sum = cache_sum.reshape(all_rows, kv_heads, groups, HEAD_WIDTH)
    cache_max = cache_max.reshape(all_rows, kv_heads, groups)
    cache_out, cache_lse = finish_group(cache_max, cache_total, cache_sum)
    window = max(local_rows, TQ)
    window_start = row_start // window * window
    row_ids = row_start + jnp.arange(local_rows, dtype=jnp.int32)
    row_request = row_ids // TQ
    key_request = (window_start + jnp.arange(window, dtype=jnp.int32)) // TQ
    reached_rows = lax.dynamic_slice_in_dim(
        ancestors(parents).reshape(all_rows, TQ), row_start, local_rows, 0
    )
    tree_seen = (jnp.tile(reached_rows, (1, window // TQ)) > 0.5) & (
        key_request[None, :] == row_request[:, None]
    )
    tree_seen = tree_seen[:, None, None, :]
    own_queries = queries.reshape(local_rows, kv_heads, groups, HEAD_WIDTH)
    tree_keys = lax.dynamic_slice_in_dim(all_keys, window_start, window, 0).reshape(
        window, kv_heads, HEAD_WIDTH
    )
    tree_values = lax.dynamic_slice_in_dim(all_values, window_start, window, 0).reshape(
        window, kv_heads, HEAD_WIDTH
    )
    tree_scores = (
        jnp.einsum("thgd,uhd->thgu", own_queries, tree_keys, preferred_element_type=jnp.float32)
        * score_scale
    )
    tree_scores = jnp.where(tree_seen, tree_scores, masked_score)
    tree_max = tree_scores.max(-1)
    tree_weights = jnp.where(tree_seen, jnp.exp(tree_scores - tree_max[..., None]), 0.0)
    tree_total = tree_weights.sum(-1)
    tree_sum = jnp.einsum(
        "thgu,uhd->thgd",
        tree_weights.astype(jnp.bfloat16),
        tree_values,
        preferred_element_type=jnp.float32,
    )
    tree_out, tree_lse = finish_group(tree_max, tree_total, tree_sum)
    seq_count = lax.axis_size("seq")
    peer_out = lax.all_to_all(cache_out, "seq", split_axis=0, concat_axis=0, tiled=True)
    peer_lse = lax.all_to_all(cache_lse, "seq", split_axis=0, concat_axis=0, tiled=True)
    peer_out = peer_out.reshape(seq_count, local_rows, kv_heads, groups, HEAD_WIDTH)
    peer_lse = peer_lse.reshape(seq_count, local_rows, kv_heads, groups)
    best = jnp.maximum(peer_lse.max(0), tree_lse)
    peer_factor = jnp.exp(peer_lse - best[None])
    tree_factor = jnp.exp(tree_lse - best)
    own_sum = (
        jnp.einsum("nthg,nthgd->thgd", peer_factor, peer_out.astype(jnp.float32))
        + tree_out.astype(jnp.float32) * tree_factor[..., None]
    )
    own_total = peer_factor.sum(0) + tree_factor
    attended = (own_sum / own_total[..., None]).astype(jnp.bfloat16).reshape(local_rows, -1)
    own_width = MODEL_WIDTH // lax.axis_size("head")
    reduced = sent_and_summed(
        jnp.einsum("kc,tk->ct", w_out, attended, preferred_element_type=jnp.float32).astype(
            jnp.bfloat16
        ),
        "head",
        0,
    )
    residual = lax.dynamic_slice_in_dim(inputs, lax.axis_index("head") * own_width, own_width, 1)
    return (residual + reduced.T).astype(jnp.bfloat16)


def solution(mesh):
    in_specs = (
        P("seq", None),
        P(),
        P(None, "head"),
        P(None, "head"),
        P(None, "head"),
        P("head", None),
        P(None, "seq", "head"),
        P(None, "seq", "head"),
        P(),
        P(),
        P(None, "seq"),
    )
    out_specs = P("seq", "head")
    return jax.shard_map(
        per_device, mesh=mesh, in_specs=in_specs, out_specs=out_specs, check_vma=False
    )
```

profile of v0, /device:TPU:1, one launch (start us, length us, event | category | flops | bytes accessed | tf_op | source)
XLA Modules:
  0.0 102.9 jit_solution(11838796836905323436)
XLA Ops:
  0.0 0.8 convert_element_type.70
  0.8 1.0 %multiply_reduce_fusion = f32[16]{0:T(128)S(1)} fusion(bf16[16,4096]{1,0:T(8,128)(2,1)} %param.11), kind=kLoop, calls=%fused_computation.46 | loop fusion | flops 196592 | bytes 131136 | tf_op jit(solution)/shard_map/reduce_sum | solution.py:88
  1.8 3.0 %convolution_convert_fusion.1 = bf16[16,512]{1,0:T(8,128)(2,1)S(1)} fusion(bf16[4096,512]{1,0:T(8,128)(2,1)} %param.13, f32[4096]{0:T(1024)S(1)} %convert_element_type.70, f32[16]{0:T(128)S(1)} %add_rsqrt_fusion, bf16[16,4096]{1,0:T(8,128)(2,1)} %param.11), kind=kOutput, calls=%fused_computation.24 | convolution fusion | flops 67379200 | bytes 4358208 | tf_op jit(solution)/shard_map/dot_general | solution.py:91
  4.8 1.2 %convolution_convert_fusion.2 = bf16[16,128]{1,0:T(8,128)(2,1)S(1)} fusion(bf16[4096,128]{1,0:T(8,128)(2,1)S(1)} %copy-done, f32[4096]{0:T(1024)S(1)} %convert_element_type.70, f32[16]{0:T(128)S(1)} %add_rsqrt_fusion, bf16[16,4096]{1,0:T(8,128)(2,1)} %param.11), kind=kOutput, calls=%fused_computation.26 | convolution fusion | flops 17041408 | bytes 1200192 | tf_op jit(solution)/shard_map/dot_general | solution.py:95
  6.0 1.6 %convolution_convert_fusion.3 = bf16[16,128]{1,0:T(8,128)(2,1)S(1)} fusion(bf16[4096,128]{1,0:T(8,128)(2,1)} %param.14, f32[4096]{0:T(1024)S(1)} %convert_element_type.70, f32[16]{0:T(128)S(1)} %add_rsqrt_fusion, bf16[16,4096]{1,0:T(8,128)(2,1)} %param.11), kind=kOutput, calls=%fused_computation.27 | convolution fusion | flops 17041408 | bytes 1200192 | tf_op jit(solution)/shard_map/dot_general | solution.py:92
  7.7 0.9 broadcast_in_dim.66
  8.6 8.6 %all-to-all-start = ((bf16[32,16,768]{2,1,0:T(8,128)(2,1)}), bf16[32,16,768]{2,1,0:T(8,128)(2,1)S(1)}, u32[]{:S(2)}, u32[]{:S(2)}) async-start(bf16[32,16,768]{2,1,0:T(8,128)(2,1)} %broadcast_in_dim.66), calls=%async_computation | async-start | bytes 1572864 | tf_op jit(solution)/shard_map/all_to_all | solution.py:24
  17.3 1.3 %convolution_minimum_fusion.5 = f32[8,64,64]{2,1,0:T(8,128)S(1)} fusion(f32[64,64]{1,0:T(8,128)S(1)} %fusion.37, s32[8,64]{1,0:T(8,128)} %param.20), kind=kOutput, calls=%fused_computation.20 | convolution fusion | flops 25296896 | bytes 149504 | tf_op jit(solution)/shard_map/rij,rjk->rik/dot_general | solution.py:61
  18.5 0.4 convolution_minimum_fusion.4
  18.9 0.4 convolution_minimum_fusion.3
  19.3 0.4 convolution_minimum_fusion.2
  19.7 0.4 convolution_minimum_fusion.1
  20.1 0.4 convolution_minimum_fusion
  20.5 0.7 broadcast_multiply_fusion
  21.4 0.7 fusion.35
  22.1 9.3 %all-to-all-done = bf16[32,16,768]{2,1,0:T(8,128)(2,1)S(1)} async-done(((bf16[32,16,768]{2,1,0:T(8,128)(2,1)}), bf16[32,16,768]{2,1,0:T(8,128)(2,1)S(1)}, u32[]{:S(2)}, u32[]{:S(2)}) %all-to-all-start) | async-done | bytes 786464 | tf_op jit(solution)/shard_map/all_to_all | solution.py:24
  31.6 4.6 %fusion.1 = (f32[8,64,4]{1,2,0:T(4,128)S(1)}, f32[8,64,4,2048]{3,1,2,0:T(8,128)S(1)}) fusion(pred[8,2048]{1,0:T(8,128)(4,1)S(1)} %fusion.35, bf16[8,2048,128]{2,1,0:T(8,128)(2,1)} %param.17, bf16[8,64,4,128]{3,2,1,0:T(4,128)(2,1)S(1)} %reshape.326), kind=kOutput, calls=%fused_computation.3 | convolution fusion | flops 1086322688 | bytes 21520384 | tf_op jit(solution)/shard_map/rthgd,rchd->rthgc/dot_general | solution.py:116
  36.2 5.7 %copy-done.1 = f32[8,64,4,2048]{3,1,2,0:T(8,128)} copy-done((f32[8,64,4,2048]{3,1,2,0:T(8,128)}, f32[8,64,4,2048]{3,1,2,0:T(8,128)S(1)}, u32[]{:S(2)}) %copy-start.1) | copy-done | bytes 16777240
  41.9 4.8 %fusion.3 = f32[8,64,4]{1,2,0:T(4,128)S(1)} fusion(f32[8,64,4,2048]{3,1,2,0:T(8,128)S(1)} %get-tuple-element.14, f32[8,64,4]{1,2,0:T(4,128)S(1)} %get-tuple-element.13, pred[8,2048]{1,0:T(8,128)(4,1)S(1)} %fusion.35), kind=kLoop, calls=%fused_computation.5 | loop fusion | flops 20969472 | bytes 16809984 | tf_op jit(solution)/shard_map/reduce_sum | solution.py:124
  46.8 0.9 copy.57
  47.6 4.0 %all-to-all-start.1 = ((f32[512,1,4]{2,1,0:T(1,128)}), f32[512,1,4]{2,1,0:T(1,128)S(1)}, u32[]{:S(2)}, u32[]{:S(2)}) async-start(f32[512,1,4]{2,1,0:T(1,128)} %bitcast.8), calls=%async_computation.1 | async-start | bytes 524288 | tf_op jit(solution)/shard_map/all_to_all | solution.py:170
  51.8 9.4 %fusion.12 = f32[8,64,1,4,128]{4,1,3,0,2:T(8,128)S(1)} fusion(bf16[8,2048,128]{2,1,0:T(8,128)(2,1)} %param.18, f32[8,64,4,2048]{3,1,2,0:T(8,128)} %copy-done.1, f32[8,64,4]{1,2,0:T(4,128)S(1)} %get-tuple-element.13, pred[8,2048]{1,0:T(8,128)(4,1)S(1)} %fusion.35), kind=kOutput, calls=%fused_computation.14 | convolution fusion | flops 1094713344 | bytes 22044672 | tf_op jit(solution)/shard_map/rthgc,rchd->rthgd/dot_general | solution.py:125
  61.2 0.3 fusion.27
  61.9 1.2 %copy.48 = bf16[512,1,4,128]{3,2,1,0:T(4,128)(2,1)} copy(bf16[512,1,4,128]{3,0,2,1:T(8,128)(2,1)S(1)} %fusion.27) | data formatting | bytes 1048576 | tf_op jit(solution)/shard_map/convert_element_type | solution.py:68
  63.1 7.5 %all-to-all-start.2 = ((bf16[512,1,4,128]{3,2,1,0:T(4,128)(2,1)}), bf16[512,1,4,128]{3,2,1,0:T(4,128)(2,1)S(1)}, u32[]{:S(2)}, u32[]{:S(2)}) async-start(bf16[512,1,4,128]{3,2,1,0:T(4,128)(2,1)} %copy.48), calls=%async_computation.2 | async-start | bytes 1048576 | tf_op jit(solution)/shard_map/all_to_all | solution.py:169
  71.6 10.5 %all-to-all-done.2 = bf16[512,1,4,128]{3,2,1,0:T(4,128)(2,1)S(1)} async-done(((bf16[512,1,4,128]{3,2,1,0:T(4,128)(2,1)}), bf16[512,1,4,128]{3,2,1,0:T(4,128)(2,1)S(1)}, u32[]{:S(2)}, u32[]{:S(2)}) %all-to-all-start.2) | async-done | bytes 524320 | tf_op jit(solution)/shard_map/all_to_all | solution.py:169
  82.1 0.4 fusion.28
  82.7 2.8 %convolution_convert_fusion = bf16[16,4096]{1,0:T(8,128)(2,1)S(1)} fusion(bf16[512,4096]{1,0:T(8,128)(2,1)} %param.16, bf16[2,8,4,128]{3,2,1,0:T(4,128)(2,1)S(1)} %bitcast.174), kind=kOutput, calls=%fused_computation.10 | convolution fusion | flops 67174400 | bytes 4341760 | tf_op jit(solution)/shard_map/kc,tk->ct/dot_general | solution.py:184
  85.6 0.7 copy.86
  86.2 8.2 %all-to-all-start.3 = ((bf16[8,512,16]{1,2,0:T(8,128)(2,1)}), bf16[8,512,16]{1,2,0:T(8,128)(2,1)S(1)}, u32[]{:S(2)}, u32[]{:S(2)}) async-start(bf16[8,512,16]{1,2,0:T(8,128)(2,1)} %bitcast.164), calls=%async_computation.3 | async-start | bytes 262144 | tf_op jit(solution)/shard_map/all_to_all | solution.py:50
  94.4 7.8 %all-to-all-done.3 = bf16[8,512,16]{1,2,0:T(8,128)(2,1)S(1)} async-done(((bf16[8,512,16]{1,2,0:T(8,128)(2,1)}), bf16[8,512,16]{1,2,0:T(8,128)(2,1)S(1)}, u32[]{:S(2)}, u32[]{:S(2)}) %all-to-all-start.3) | async-done | bytes 131104 | tf_op jit(solution)/shard_map/all_to_all | solution.py:50
  102.3 0.6 fusion.36
  (35 shorter events, 2.1 us)
Async XLA Ops:
  0.0 4.8 %copy-start = (bf16[4096,128]{1,0:T(8,128)(2,1)S(1)}, bf16[4096,128]{1,0:T(8,128)(2,1)}, u32[]{:S(2)}) copy-start(bf16[4096,128]{1,0:T(8,128)(2,1)} %param.15) | copy-start | bytes 3145732
  8.6 22.8 %all-to-all-start = ((bf16[32,16,768]{2,1,0:T(8,128)(2,1)}), bf16[32,16,768]{2,1,0:T(8,128)(2,1)S(1)}, u32[]{:S(2)}, u32[]{:S(2)}) async-start(bf16[32,16,768]{2,1,0:T(8,128)(2,1)} %broadcast_in_dim.66), calls=%async_computation | async-start | bytes 1572864 | tf_op jit(solution)/shard_map/all_to_all | solution.py:24
  36.2 5.7 %copy-start.1 = (f32[8,64,4,2048]{3,1,2,0:T(8,128)}, f32[8,64,4,2048]{3,1,2,0:T(8,128)S(1)}, u32[]{:S(2)}) copy-start(f32[8,64,4,2048]{3,1,2,0:T(8,128)S(1)} %get-tuple-element.14) | copy-start | bytes 50331652
  47.6 15.5 %all-to-all-start.1 = ((f32[512,1,4]{2,1,0:T(1,128)}), f32[512,1,4]{2,1,0:T(1,128)S(1)}, u32[]{:S(2)}, u32[]{:S(2)}) async-start(f32[512,1,4]{2,1,0:T(1,128)} %bitcast.8), calls=%async_computation.1 | async-start | bytes 524288 | tf_op jit(solution)/shard_map/all_to_all | solution.py:170
  51.7 42.6 %copy-start.2 = (bf16[16,4096]{1,0:T(8,128)(2,1)S(1)}, bf16[16,4096]{1,0:T(8,128)(2,1)}, u32[]{:S(2)}) copy-start(bf16[16,4096]{1,0:T(8,128)(2,1)} %param.11) | copy-start | bytes 393220
  63.1 18.9 %all-to-all-start.2 = ((bf16[512,1,4,128]{3,2,1,0:T(4,128)(2,1)}), bf16[512,1,4,128]{3,2,1,0:T(4,128)(2,1)S(1)}, u32[]{:S(2)}, u32[]{:S(2)}) async-start(bf16[512,1,4,128]{3,2,1,0:T(4,128)(2,1)} %copy.48), calls=%async_computation.2 | async-start | bytes 1048576 | tf_op jit(solution)/shard_map/all_to_all | solution.py:169
  86.2 16.0 %all-to-all-start.3 = ((bf16[8,512,16]{1,2,0:T(8,128)(2,1)}), bf16[8,512,16]{1,2,0:T(8,128)(2,1)S(1)}, u32[]{:S(2)}, u32[]{:S(2)}) async-start(bf16[8,512,16]{1,2,0:T(8,128)(2,1)} %bitcast.164), calls=%async_computation.3 | async-start | bytes 262144 | tf_op jit(solution)/shard_map/all_to_all | solution.py:50
where the time goes:
time: 104 us; the launch traced here: 103 us
  starting transfers between devices  28.3 us (27%)
  waiting for transfers between devices  27.6 us (27%)
  matrix products  26.6 us (26%)
  local copies, waits for them, and re-layouts  10.5 us (10%)
  other arithmetic  9.54 us (9%)
    all_to_all x1, waiting for transfers between devices, per_device(): lax.all_to_all(cache_out, 'seq', split_axis=0, concat_axis=0, tiled=True)  10.5 us
    dot_general x1, matrix products, per_device(): jnp.einsum('rthgc,rchd->rthgd', cache_weights.astype(jnp.bfloat16), value...  9.35 us
    all_to_all x1, waiting for transfers between devices, sent_to_all(): lax.all_to_all(jnp.broadcast_to(array[None], (size, *array.shape)), axis,...  9.32 us
    all_to_all x1, starting transfers between devices, sent_to_all(): lax.all_to_all(jnp.broadcast_to(array[None], (size, *array.shape)), axis,...  8.58 us
    all_to_all x1, starting transfers between devices, sent_and_summed(): lax.all_to_all(blocks, axis, split_axis=0, concat_axis=0, tiled=True)  8.18 us
    all_to_all x1, waiting for transfers between devices, sent_and_summed(): lax.all_to_all(blocks, axis, split_axis=0, concat_axis=0, tiled=True)  7.82 us
    all_to_all x1, starting transfers between devices, per_device(): lax.all_to_all(cache_out, 'seq', split_axis=0, concat_axis=0, tiled=True)  7.49 us
    unnamed x7, local copies, waits for them, and re-layouts  5.8 us
  transfers between devices with their start and end apart: 4, of which 3 were waited for; matrix products, arithmetic and copies ran while one was open for 17% of the time, Pallas kernels for 0%

commit v1 on v0

v1 whole, which is shorter than its diff:
```python
import functools
import math

import jax
import jax.numpy as jnp
from jax import lax
from jax.experimental import pallas as pl
from jax.experimental.pallas import tpu as pltpu
from jax.sharding import PartitionSpec as P

NORM_EPSILON = 1e-05
HIDDEN = -1e30
HEAD_WIDTH = 128
TREE = 64
PAGE = 128
KEY_TILE = 256
WEIGHT_PARTS = 4

NT = (((1,), (1,)), ((), ()))
TN = (((0,), (0,)), ((), ()))
F32 = jnp.float32
BF16 = jnp.bfloat16


def layer(
    n_seq,
    n_head,
    lengths_ref,
    slots_ref,
    tokens_ref,
    gain_ref,
    parents_ref,
    wq_hbm,
    wk_hbm,
    wv_hbm,
    wo_hbm,
    keys_hbm,
    values_hbm,
    mixed_ref,
    wqkv,
    wo,
    keys,
    values,
    normed,
    qall,
    kvtree,
    score_a,
    score_b,
    top_a,
    top_b,
    out_send,
    lse_send,
    out_recv,
    lse_recv,
    part_send,
    part_recv,
    w_sem,
    wo_sem,
    k_sem,
    v_sem,
    q_send_sem,
    q_recv_sem,
    kv_send_sem,
    kv_recv_sem,
    o_send_sem,
    o_recv_sem,
    l_send_sem,
    l_recv_sem,
    p_send_sem,
    p_recv_sem,
):
    me = lax.axis_index("seq")
    head = lax.axis_index("head")
    rows, width = tokens_ref.shape
    requests = keys.shape[0]
    context = keys.shape[1]
    owners = TREE // rows
    q_width = wq_hbm.shape[1]
    groups = q_width // HEAD_WIDTH
    block = groups * rows
    queries = owners * block
    tiles = context // KEY_TILE
    own_request = me // owners
    own_place = me % owners
    scale = HEAD_WIDTH**-0.5
    scale2 = scale * math.log2(math.e)

    part = width // WEIGHT_PARTS

    def weight_copies(c):
        at = pl.ds(c * part, part)
        return (
            pltpu.make_async_copy(
                wq_hbm.at[at], wqkv.at[at, pl.ds(0, q_width)], w_sem.at[0, c]
            ),
            pltpu.make_async_copy(
                wk_hbm.at[at], wqkv.at[at, pl.ds(q_width, HEAD_WIDTH)], w_sem.at[1, c]
            ),
            pltpu.make_async_copy(
                wv_hbm.at[at],
                wqkv.at[at, pl.ds(q_width + HEAD_WIDTH, HEAD_WIDTH)],
                w_sem.at[2, c],
            ),
        )

    def key_copy(r):
        return pltpu.make_async_copy(keys_hbm.at[r], keys.at[r], k_sem.at[r])

    def value_copy(r):
        return pltpu.make_async_copy(values_hbm.at[r], values.at[r], v_sem.at[r])

    own_width = width // n_head

    def wo_copy(j):
        at = pl.ds(pl.multiple_of(j * own_width, own_width), own_width)
        return pltpu.make_async_copy(wo_hbm.at[:, at], wo.at[j], wo_sem.at[j])

    def request_at(i):
        return (own_request + i) % requests

    for c in range(WEIGHT_PARTS):
        for copy in weight_copies(c):
            copy.start()

    def start_cache(i, _):
        key_copy(request_at(i)).start()
        value_copy(request_at(i)).start()
        return 0

    lax.fori_loop(1, requests + 1, start_cache, 0)

    def start_wo(j, _):
        wo_copy(j).start()
        return 0

    lax.fori_loop(0, n_head, start_wo, 0)

    barrier = pltpu.get_barrier_semaphore()

    def greet_seq(j, _):
        pl.semaphore_signal(
            barrier,
            inc=1,
            device_id=((me + j) % n_seq, head),
            device_id_type=pl.DeviceIdType.MESH,
        )
        return 0

    def greet_head(j, _):
        pl.semaphore_signal(
            barrier,
            inc=1,
            device_id=(me, (head + j) % n_head),
            device_id_type=pl.DeviceIdType.MESH,
        )
        return 0

    lax.fori_loop(1, n_seq, greet_seq, 0)
    lax.fori_loop(1, n_head, greet_head, 0)

    inputs = tokens_ref[...].astype(F32)
    mean = jnp.mean(inputs * inputs, axis=-1, keepdims=True)
    normed[...] = (
        inputs * lax.rsqrt(mean + NORM_EPSILON) * gain_ref[...].astype(F32)
    ).astype(BF16)

    parent = parents_ref[pl.ds(own_request, 1), :]
    node = lax.broadcasted_iota(jnp.int32, (TREE, TREE), 0)
    other = lax.broadcasted_iota(jnp.int32, (TREE, TREE), 1)
    reached = jnp.where((parent == node) | (node == other), 1.0, 0.0)
    for _ in range(max(1, (TREE - 1).bit_length())):
        half = reached.astype(BF16)
        reached = jnp.minimum(jnp.dot(half, half, preferred_element_type=F32), 1.0)

    projected = jnp.zeros((rows, wqkv.shape[1]), F32)
    for c in range(WEIGHT_PARTS):
        for copy in weight_copies(c):
            copy.wait()
        projected += jnp.dot(
            normed[:, c * part : (c + 1) * part],
            wqkv[c * part : (c + 1) * part, :],
            preferred_element_type=F32,
        )
    projected = projected.astype(BF16)
    for g in range(groups):
        qall[me, g * rows : (g + 1) * rows, :] = projected[
            :, g * HEAD_WIDTH : (g + 1) * HEAD_WIDTH
        ]
    for n in range(2):
        kvtree[own_place, n * rows : (n + 1) * rows, :] = projected[
            :, q_width + n * HEAD_WIDTH : q_width + (n + 1) * HEAD_WIDTH
        ]

    def q_copy(peer):
        return pltpu.make_async_remote_copy(
            src_ref=qall.at[me],
            dst_ref=qall.at[me],
            send_sem=q_send_sem,
            recv_sem=q_recv_sem.at[own_request],
            device_id=(peer, head),
            device_id_type=pl.DeviceIdType.MESH,
        )

    pl.semaphore_wait(barrier, n_seq - 1 + n_head - 1)

    def kv_send(j, _):
        peer = own_request * owners + (own_place + j) % owners
        pltpu.make_async_remote_copy(
            src_ref=kvtree.at[own_place],
            dst_ref=kvtree.at[own_place],
            send_sem=kv_send_sem,
            recv_sem=kv_recv_sem,
            device_id=(peer, head),
            device_id_type=pl.DeviceIdType.MESH,
        ).start()
        return 0

    def q_send(n, _):
        to = (own_request + requests - 1 - n // owners) % requests
        q_copy(to * owners + (own_place + n) % owners).start()
        return 0

    def q_send_own(j, _):
        q_copy(own_request * owners + (own_place + j) % owners).start()
        return 0

    lax.fori_loop(0, owners, q_send, 0)
    lax.fori_loop(1, owners, kv_send, 0)
    lax.fori_loop(owners, (requests - 1) * owners, q_send, 0)
    lax.fori_loop(1, owners, q_send_own, 0)

    pltpu.make_async_copy(
        kvtree.at[pl.ds(0, owners - 1)], kvtree.at[pl.ds(0, owners - 1)], kv_recv_sem
    ).wait()
    lanes = 128
    own_queries = qall[me]
    own_queries = jnp.concatenate([own_queries] * (lanes // block), axis=0)
    tree_keys = kvtree[:, :rows, :].reshape(TREE, HEAD_WIDTH)
    tree_values = kvtree[:, rows:, :].reshape(TREE, HEAD_WIDTH)
    token = lax.broadcasted_iota(jnp.int32, (TREE, lanes), 0)
    lane = lax.broadcasted_iota(jnp.int32, (TREE, lanes), 1)
    pick = jnp.where(token == own_place * rows + lane % rows, 1.0, 0.0).astype(BF16)
    seen = jnp.dot(reached.astype(BF16), pick, preferred_element_type=F32) > 0.5
    tree_scores = lax.dot_general(
        tree_keys, own_queries, NT, preferred_element_type=F32
    )
    tree_scores = jnp.where(seen, tree_scores, HIDDEN)
    tree_top = jnp.max(tree_scores, axis=0, keepdims=True)
    tree_weights = jnp.where(
        seen, jnp.exp2(tree_scores * scale2 - tree_top * scale2), 0.0
    )
    tree_total = jnp.maximum(jnp.sum(tree_weights, axis=0, keepdims=True), 1.0)
    tree_sum = lax.dot_general(
        tree_values, tree_weights.astype(BF16), TN, preferred_element_type=F32
    )
    tree_out = (tree_sum / tree_total).astype(BF16).astype(F32).T[:block]
    tree_lse = tree_top * scale + jnp.log(tree_total)

    row_in_page = lax.broadcasted_iota(jnp.int32, (PAGE, queries), 0)

    def wait_for(i):
        r = request_at(i)

        @pl.when(i < requests)
        def _():
            at = pl.ds(r * owners, owners)
            pltpu.make_async_copy(qall.at[at], qall.at[at], q_recv_sem.at[r]).wait()

        @pl.when(i == requests)
        def _():
            at = pl.ds(r * owners, owners - 1)
            pltpu.make_async_copy(qall.at[at], qall.at[at], q_recv_sem.at[r]).wait()

        key_copy(r).wait()

    def score_tile(i, b, best, score):
        r = request_at(i)
        q = qall[pl.ds(r * owners, owners)].reshape(queries, HEAD_WIDTH)
        s = lax.dot_general(
            keys[r, b * KEY_TILE : (b + 1) * KEY_TILE, :],
            q,
            NT,
            preferred_element_type=F32,
        )
        for n in range(KEY_TILE // PAGE):
            p = b * (KEY_TILE // PAGE) + n
            left = lengths_ref[r] - slots_ref[r, p] * PAGE
            shown = jnp.where(
                row_in_page < left, s[n * PAGE : (n + 1) * PAGE], HIDDEN
            )
            score[p * PAGE : (p + 1) * PAGE, :] = shown
            high = jnp.max(shown.reshape(PAGE // 8, 8, queries), axis=0)
            best = high if best is None else jnp.maximum(best, high)
        return best

    def weigh_tile(i, b, state, score, top):
        r = request_at(i)
        acc, total = state
        w = jnp.exp2(score[b * KEY_TILE : (b + 1) * KEY_TILE, :] * scale2 - top)
        low = jnp.sum(w.reshape(KEY_TILE // 8, 8, queries), axis=0)
        added = lax.dot_general(
            values[r, b * KEY_TILE : (b + 1) * KEY_TILE, :],
            w.astype(BF16),
            TN,
            preferred_element_type=F32,
        )
        if acc is None:
            return added, low
        return acc + added, total + low

    def finish(i, state, top):
        acc, total = state
        total = jnp.maximum(jnp.sum(total, axis=0, keepdims=True), 1.0)
        out = (acc / total).T.astype(BF16)
        out_send[i - 1] = out.reshape(owners, block, HEAD_WIDTH)
        lse = top * (1.0 / math.log2(math.e)) + jnp.log(total)
        lse_send[i - 1] = jnp.concatenate(
            [lse[:, n * 128 : (n + 1) * 128] for n in range(queries // 128)], axis=0
        )

    def send_out(i):
        r = request_at(i)

        def send(peer_place):
            peer = r * owners + peer_place
            pltpu.make_async_remote_copy(
                src_ref=out_send.at[i - 1, peer_place],
                dst_ref=out_recv.at[me],
                send_sem=o_send_sem,
                recv_sem=o_recv_sem,
                device_id=(peer, head),
                device_id_type=pl.DeviceIdType.MESH,
            ).start()
            pltpu.make_async_remote_copy(
                src_ref=lse_send.at[i - 1],
                dst_ref=lse_recv.at[me],
                send_sem=l_send_sem,
                recv_sem=l_recv_sem,
                device_id=(peer, head),
                device_id_type=pl.DeviceIdType.MESH,
            ).start()

        for j in range(owners):
            place = (own_place + j) % owners
            if j == 0:

                @pl.when(i < requests)
                def _():
                    send(place)

            else:
                send(place)

    def half_step(i, now, after):
        score, top_ref = now
        wait_value = value_copy(request_at(i))
        wait_value.wait()
        top = jnp.max(top_ref[...], axis=0, keepdims=True) * scale2
        state = (None, None)
        best = None
        for b in range(tiles):
            if after is not None:
                best = score_tile(i + 1, b, best, after[0])
            state = weigh_tile(i, b, state, score, top)
        if after is not None:
            after[1][...] = best
        finish(i, state, top)
        send_out(i)

    a, b = (score_a, top_a), (score_b, top_b)
    wait_for(1)
    best = None
    for t in range(tiles):
        best = score_tile(1, t, best, score_a)
    top_a[...] = best

    def two_steps(n, _):
        i = 1 + 2 * n
        wait_for(i + 1)
        half_step(i, a, b)
        wait_for(i + 2)
        half_step(i + 1, b, a)
        return 0

    lax.fori_loop(0, requests // 2 - 1, two_steps, 0)
    wait_for(requests)
    half_step(requests - 1, a, b)
    half_step(requests, b, None)
    out_recv[me] = out_send[requests - 1, own_place]
    lse_recv[me] = lse_send[requests - 1]

    def arrived(ref, count, sem):
        at = pl.ds(0, count)
        pltpu.make_async_copy(ref.at[at], ref.at[at], sem).wait()

    arrived(lse_recv, n_seq - 1, l_recv_sem)
    per_line = 128 // block
    lse = lse_recv[:, pl.ds(own_place // per_line, 1), :].reshape(n_seq, 128)
    lse = pltpu.roll(lse, (128 - (own_place % per_line) * block) % 128, 1)
    best = jnp.maximum(jnp.max(lse, axis=0, keepdims=True), tree_lse)
    factor = jnp.exp(lse - best)
    tree_factor = jnp.exp(tree_lse - best)
    total = jnp.sum(factor, axis=0, keepdims=True) + tree_factor
    factor = jnp.concatenate(
        [factor / total, jnp.broadcast_to(tree_factor / total, (8, 128))], axis=0
    ).T[:block]
    for j in range(n_head):
        wo_copy(j).wait()
    arrived(out_recv, n_seq - 1, o_recv_sem)
    merged = tree_out * factor[:, n_seq : n_seq + 1]
    for n in range(n_seq):
        merged += out_recv[n].astype(F32) * factor[:, n : n + 1]
    merged = merged.astype(BF16)
    attended = jnp.concatenate(
        [merged[g * rows : (g + 1) * rows] for g in range(groups)], axis=1
    )

    def piece(j):
        return jnp.dot(attended, wo[j], preferred_element_type=F32)

    def part_copy(j):
        return pltpu.make_async_remote_copy(
            src_ref=part_send.at[j],
            dst_ref=part_recv.at[head],
            send_sem=p_send_sem,
            recv_sem=p_recv_sem,
            device_id=(me, j),
            device_id_type=pl.DeviceIdType.MESH,
        )

    order = sorted(range(1, n_head), key=lambda d: -min(d, n_head - d))
    for n, d in enumerate(order):
        j = (head + d) % n_head
        part_send[j] = piece(j).astype(BF16)
        if n > 0:
            part_copy((head + order[n - 1]) % n_head).start()
    mine = piece(head)
    part_copy((head + order[-1]) % n_head).start()
    at = pl.ds(pl.multiple_of(head * own_width, own_width), own_width)
    mine = mine + tokens_ref[:, at].astype(F32)
    part_recv[head] = jnp.zeros((rows, own_width), BF16)
    arrived(part_recv, n_head - 1, p_recv_sem)
    mixed_ref[...] = (mine + jnp.sum(part_recv[...].astype(F32), axis=0)).astype(BF16)

    arrived(part_send, n_head - 1, p_send_sem)
    arrived(qall, n_seq - 1, q_send_sem)
    arrived(kvtree, owners - 1, kv_send_sem)
    arrived(out_recv, n_seq - 1, o_send_sem)
    arrived(lse_recv, n_seq - 1, l_send_sem)


def per_device(
    tokens,
    norm_gain,
    w_query,
    key_projection,
    value_projection,
    w_out,
    cache_keys,
    paged_value_cache,
    lengths,
    parents,
    slot_block,
):
    n_seq = lax.axis_size("seq")
    n_head = lax.axis_size("head")
    rows, width = tokens.shape
    requests, context, _ = cache_keys.shape
    q_width = w_query.shape[1]
    groups = q_width // HEAD_WIDTH
    owners = TREE // rows
    block = groups * rows
    queries = owners * block
    own_width = width // n_head
    vmem = pl.BlockSpec(memory_space=pltpu.VMEM)
    smem = pl.BlockSpec(memory_space=pltpu.SMEM)
    hbm = pl.BlockSpec(memory_space=pl.ANY)
    dma = pltpu.SemaphoreType.DMA
    return pl.pallas_call(
        functools.partial(layer, n_seq, n_head),
        out_shape=jax.ShapeDtypeStruct((rows, own_width), BF16),
        in_specs=[smem, smem, vmem, vmem, vmem, hbm, hbm, hbm, hbm, hbm, hbm],
        out_specs=vmem,
        scratch_shapes=[
            pltpu.VMEM((width, q_width + 2 * HEAD_WIDTH), BF16),
            pltpu.VMEM((n_head, q_width, own_width), BF16),
            pltpu.VMEM((requests, context, HEAD_WIDTH), BF16),
            pltpu.VMEM((requests, context, HEAD_WIDTH), BF16),
            pltpu.VMEM((rows, width), BF16),
            pltpu.VMEM((n_seq, block, HEAD_WIDTH), BF16),
            pltpu.VMEM((owners, 2 * rows, HEAD_WIDTH), BF16),
            pltpu.VMEM((context, queries), F32),
            pltpu.VMEM((context, queries), F32),
            pltpu.VMEM((8, queries), F32),
            pltpu.VMEM((8, queries), F32),
            pltpu.VMEM((requests, owners, block, HEAD_WIDTH), BF16),
            pltpu.VMEM((requests, queries // 128, 128), F32),
            pltpu.VMEM((n_seq, block, HEAD_WIDTH), BF16),
            pltpu.VMEM((n_seq, queries // 128, 128), F32),
            pltpu.VMEM((n_head, rows, own_width), BF16),
            pltpu.VMEM((n_head, rows, own_width), BF16),
            dma((3, WEIGHT_PARTS)),
            dma((n_head,)),
            dma((requests,)),
            dma((requests,)),
            dma,
            dma((requests,)),
            dma,
            dma,
            dma,
            dma,
            dma,
            dma,
            dma,
            dma,
        ],
        compiler_params=pltpu.CompilerParams(
            collective_id=0,
            has_side_effects=True,
            vmem_limit_bytes=60 * 1024 * 1024,
        ),
        name="layer",
    )(
        lengths,
        slot_block,
        tokens,
        norm_gain.reshape(1, width),
        parents,
        w_query,
        key_projection,
        value_projection,
        w_out,
        cache_keys,
        paged_value_cache,
    )


def solution(mesh):
    in_specs = (
        P("seq", None),
        P(),
        P(None, "head"),
        P(None, "head"),
        P(None, "head"),
        P("head", None),
        P(None, "seq", "head"),
        P(None, "seq", "head"),
        P(),
        P(),
        P(None, "seq"),
    )
    return jax.shard_map(
        per_device,
        mesh=mesh,
        in_specs=in_specs,
        out_specs=P("seq", "head"),
        check_vma=False,
    )
```

time: 104 us -> 39.1 us (0.38)
  Pallas kernels: 0 us -> 35.9 us
  starting transfers between devices: 28.3 us -> 0 us
  waiting for transfers between devices: 27.6 us -> 0 us
  matrix products: 26.6 us -> 0 us
  other arithmetic: 9.54 us -> 0 us
  local copies, waits for them, and re-layouts: 10.5 us -> 2.64 us
    pallas_call x0 -> x1, Pallas kernels: none -> 35.9 us  [per_device(): pl.pallas_call(functools.partial(layer, n_seq, n_head), out_shape=jax.Sha...]
    all_to_all x4 -> x0, starting transfers between devices: 28.3 us -> none  [the longest x1 8.58 us: sent_to_all(): lax.all_to_all(jnp.broadcast_to(array[None], (size, *array.shape)), axis,...]
    all_to_all x4 -> x0, waiting for transfers between devices: 27.6 us -> none  [the longest x1 10.5 us: per_device(): lax.all_to_all(cache_out, 'seq', split_axis=0, concat_axis=0, tiled=True)]
    dot_general x15 -> x0, matrix products: 26.6 us -> none  [the longest x1 9.35 us: per_device(): jnp.einsum('rthgc,rchd->rthgd', cache_weights.astype(jnp.bfloat16), value...]
    reduce_sum x5 -> x0, other arithmetic: 6.1 us -> none  [the longest x1 4.82 us: per_device(): cache_total = cache_weights.sum(-1).reshape(all_rows, kv_heads, groups)]
    unnamed x7 -> x1, local copies, waits for them, and re-layouts: 5.8 us -> 1.32 us
    convert_element_type x5 -> x0, other arithmetic: 1.78 us -> none  [the longest x1 0.79 us: per_device(): norm_gain.astype(jnp.float32)]
    convert_element_type x2 -> x0, local copies, waits for them, and re-layouts: 1.21 us -> none  [the longest x1 1.21 us: finish_group(): output = (group_sum / floored[..., None]).astype(jnp.bfloat16)]
  transfers between devices with their start and end apart: 4 -> 0, of which waited for: 3 -> 0; matrix products, arithmetic and copies ran while one was open for 17% -> 0% of each run, Pallas kernels for 0% -> 0%
where the time goes in v1:
time: 39.1 us; the launch traced here: 38.6 us
  Pallas kernels  35.9 us (92%)
  local copies, waits for them, and re-layouts  2.64 us (7%)
    pallas_call x1, Pallas kernels, per_device(): pl.pallas_call(functools.partial(layer, n_seq, n_head), out_shape=jax.Sha...  35.9 us
    unnamed x1, local copies, waits for them, and re-layouts  1.32 us
    reshape x1, local copies, waits for them, and re-layouts, per_device(): norm_gain.reshape(1, width)  1.31 us

profile of v1, /device:TPU:1, one launch (start us, length us, event | category | flops | bytes accessed | tf_op | source)
XLA Modules:
  0.0 38.6 jit_solution(13467877972230432599)
XLA Ops:
  0.0 1.3 %reshape.3.gain_ref = bf16[1,4096]{1,0:T(2,128)(2,1)} reshape(bf16[4096]{0:T(1024)(128)(2,1)} %param.12) | data formatting | bytes 16384 | tf_op jit(solution)/shard_map/reshape | solution.py:527
  1.3 35.9 %layer.1 = bf16[16,512]{1,0:T(8,128)(2,1)} custom-call(s32[8]{0:T(128)} %lengths_ref.1, s32[8,16]{1,0:T(8,128)} %slots_ref.1, bf16[16,4096]{1,0:T(8,128)(2,1)} %tokens_ref.1, bf16[1,4096]{1,0:T(2,128)(2,1)} %reshape.3.gain_ref, s32[8,64]{1,0:T(8,128)} %parents_ref.1, bf16[4096,512]{1,0:T(8,128)(2,1)} %wq_hbm.1, bf16[4096,128]{1,0:T(8,128)(2,1)} %wk_hbm.1, ...), custom_call_target="tpu_custom_call" | custom-call | tf_op jit(solution)/shard_map/layer/pallas_call | solution.py:479
  37.3 1.3 %copy.13 = bf16[16,512]{1,0:T(8,128)(2,1)} copy(bf16[16,512]{1,0:T(8,128)(2,1)} %layer.1) | data formatting | bytes 32768

commit v2 on v1

--- a/solution.py
+++ b/solution.py
@@ -25,11 +25,11 @@
 def layer(
     n_seq,
     n_head,
-    lengths_ref,
-    slots_ref,
-    tokens_ref,
-    gain_ref,
-    parents_ref,
+    lengths_hbm,
+    slots_hbm,
+    tokens_hbm,
+    gain_hbm,
+    parents_hbm,
     wq_hbm,
     wk_hbm,
     wv_hbm,
@@ -37,6 +37,12 @@
     keys_hbm,
     values_hbm,
     mixed_ref,
+    lengths_ref,
+    slots_ref,
+    tokens_ref,
+    gain_ref,
+    parents_ref,
+    small_sem,
     wqkv,
     wo,
     keys,
@@ -85,6 +91,43 @@
     scale = HEAD_WIDTH**-0.5
     scale2 = scale * math.log2(math.e)
 
+    barrier = pltpu.get_barrier_semaphore()
+
+    def greet_seq(j, _):
+        pl.semaphore_signal(
+            barrier,
+            inc=1,
+            device_id=((me + j) % n_seq, head),
+            device_id_type=pl.DeviceIdType.MESH,
+        )
+        return 0
+
+    def greet_head(j, _):
+        pl.semaphore_signal(
+            barrier,
+            inc=1,
+            device_id=(me, (head + j) % n_head),
+            device_id_type=pl.DeviceIdType.MESH,
+        )
+        return 0
+
+    lax.fori_loop(1, n_seq, greet_seq, 0)
+    lax.fori_loop(1, n_head, greet_head, 0)
+
+    small = [
+        pltpu.make_async_copy(source, target, small_sem.at[n])
+        for n, (source, target) in enumerate(
+            (
+                (tokens_hbm, tokens_ref),
+                (gain_hbm, gain_ref),
+                (parents_hbm, parents_ref),
+                (lengths_hbm, lengths_ref),
+                (slots_hbm, slots_ref),
+            )
+        )
+    ]
+    for copy in small:
+        copy.start()
     part = width // WEIGHT_PARTS
 
     def weight_copies(c):
@@ -127,43 +170,22 @@
         value_copy(request_at(i)).start()
         return 0
 
-    lax.fori_loop(1, requests + 1, start_cache, 0)
-
     def start_wo(j, _):
         wo_copy(j).start()
         return 0
 
-    lax.fori_loop(0, n_head, start_wo, 0)
-
-    barrier = pltpu.get_barrier_semaphore()
-
-    def greet_seq(j, _):
-        pl.semaphore_signal(
-            barrier,
-            inc=1,
-            device_id=((me + j) % n_seq, head),
-            device_id_type=pl.DeviceIdType.MESH,
-        )
-        return 0
-
-    def greet_head(j, _):
-        pl.semaphore_signal(
-            barrier,
-            inc=1,
-            device_id=(me, (head + j) % n_head),
-            device_id_type=pl.DeviceIdType.MESH,
-        )
-        return 0
-
-    lax.fori_loop(1, n_seq, greet_seq, 0)
-    lax.fori_loop(1, n_head, greet_head, 0)
-
+    small[0].wait()
+    small[1].wait()
     inputs = tokens_ref[...].astype(F32)
     mean = jnp.mean(inputs * inputs, axis=-1, keepdims=True)
     normed[...] = (
-        inputs * lax.rsqrt(mean + NORM_EPSILON) * gain_ref[...].astype(F32)
+        inputs
+        * lax.rsqrt(mean + NORM_EPSILON)
+        * gain_ref[...].reshape(1, width).astype(F32)
     ).astype(BF16)
 
+    for copy in small[2:]:
+        copy.wait()
     parent = parents_ref[pl.ds(own_request, 1), :]
     node = lax.broadcasted_iota(jnp.int32, (TREE, TREE), 0)
     other = lax.broadcasted_iota(jnp.int32, (TREE, TREE), 1)
@@ -176,6 +198,9 @@
     for c in range(WEIGHT_PARTS):
         for copy in weight_copies(c):
             copy.wait()
+        if c == WEIGHT_PARTS - 1:
+            lax.fori_loop(1, requests + 1, start_cache, 0)
+            lax.fori_loop(0, n_head, start_wo, 0)
         projected += jnp.dot(
             normed[:, c * part : (c + 1) * part],
             wqkv[c * part : (c + 1) * part, :],
@@ -473,15 +498,20 @@
     queries = owners * block
     own_width = width // n_head
     vmem = pl.BlockSpec(memory_space=pltpu.VMEM)
-    smem = pl.BlockSpec(memory_space=pltpu.SMEM)
-    hbm = pl.BlockSpec(memory_space=pl.ANY)
+    hbm = pl.BlockSpec(memory_space=pltpu.HBM)
     dma = pltpu.SemaphoreType.DMA
     return pl.pallas_call(
         functools.partial(layer, n_seq, n_head),
-        out_shape=jax.ShapeDtypeStruct((rows, own_width), BF16),
-        in_specs=[smem, smem, vmem, vmem, vmem, hbm, hbm, hbm, hbm, hbm, hbm],
+        out_shape=pltpu.VMEM((rows, own_width), BF16),
+        in_specs=[hbm] * 11,
         out_specs=vmem,
         scratch_shapes=[
+            pltpu.SMEM(lengths.shape, jnp.int32),
+            pltpu.SMEM(slot_block.shape, jnp.int32),
+            pltpu.VMEM(tokens.shape, BF16),
+            pltpu.VMEM(norm_gain.shape, BF16),
+            pltpu.VMEM(parents.shape, jnp.int32),
+            dma((5,)),
             pltpu.VMEM((width, q_width + 2 * HEAD_WIDTH), BF16),
             pltpu.VMEM((n_head, q_width, own_width), BF16),
             pltpu.VMEM((requests, context, HEAD_WIDTH), BF16),
@@ -524,7 +554,7 @@
         lengths,
         slot_block,
         tokens,
-        norm_gain.reshape(1, width),
+        norm_gain,
         parents,
         w_query,
         key_projection,

time: 39.1 us -> 36.9 us (0.944); the launches traced: 38.6 us -> 36.9 us
  local copies, waits for them, and re-layouts: 2.64 us -> 0.61 us
    reshape x1 -> x0, local copies, waits for them, and re-layouts: 1.31 us -> none  [per_device(): norm_gain.reshape(1, width)]
    unnamed x1, local copies, waits for them, and re-layouts: 1.32 us -> 0.61 us
where the time goes in v2:
time: 36.9 us
  Pallas kernels  36.2 us (98%)
  local copies, waits for them, and re-layouts  0.61 us (2%)
    pallas_call x1, Pallas kernels, per_device(): pl.pallas_call(functools.partial(layer, n_seq, n_head), out_shape=pltpu.V...  36.2 us

profile of v2, /device:TPU:1, one launch (start us, length us, event | category | flops | bytes accessed | tf_op | source)
XLA Modules:
  0.0 36.9 jit_solution(18099204127139433245)
XLA Ops:
  0.0 36.2 %layer.1 = bf16[16,512]{1,0:T(8,128)(2,1)S(1)} custom-call(s32[8]{0:T(128)} %lengths_hbm.1, s32[8,16]{1,0:T(8,128)} %slots_hbm.1, bf16[16,4096]{1,0:T(8,128)(2,1)} %tokens_hbm.1, bf16[4096]{0:T(1024)(128)(2,1)} %gain_hbm.1, s32[8,64]{1,0:T(8,128)} %parents_hbm.1, bf16[4096,512]{1,0:T(8,128)(2,1)} %wq_hbm.1, bf16[4096,128]{1,0:T(8,128)(2,1)} %wk_hbm.1, ...), custom_call_target="tpu_custom_call" | custom-call | tf_op jit(solution)/shard_map/layer/pallas_call | solution.py:503
  36.2 0.6 %copy.13 = bf16[16,512]{1,0:T(8,128)(2,1)} copy(bf16[16,512]{1,0:T(8,128)(2,1)S(1)} %layer.1) | data formatting | bytes 32768

commit v3 on v2

v3 whole, which is shorter than its diff:
```python
import functools
import math

import jax
import jax.numpy as jnp
from jax import lax
from jax.experimental import pallas as pl
from jax.experimental.pallas import tpu as pltpu
from jax.sharding import PartitionSpec as P

NORM_EPSILON = 1e-05
HIDDEN = -1e30
HEAD_WIDTH = 128
TREE = 64
PAGE = 128
KEY_TILE = 256
WEIGHT_PARTS = 4
ORDER = ((0, 1), (1, 0), (2, 0), (2, 1), (3, 1), (1, 1), (3, 0), (0, 0))

NT = (((1,), (1,)), ((), ()))
TN = (((0,), (0,)), ((), ()))
F32 = jnp.float32
BF16 = jnp.bfloat16


def layer(
    n_seq,
    n_head,
    lengths_hbm,
    slots_hbm,
    tokens_hbm,
    gain_hbm,
    parents_hbm,
    wq_hbm,
    wk_hbm,
    wv_hbm,
    wo_hbm,
    keys_hbm,
    values_hbm,
    mixed_ref,
    lengths_ref,
    slots_ref,
    tokens_ref,
    gain_ref,
    parents_ref,
    small_sem,
    wqkv,
    wo,
    keys,
    values,
    normed,
    qall,
    kvtree,
    score_a,
    score_b,
    top_a,
    top_b,
    out_own,
    lse_own,
    out_swap,
    lse_swap,
    out_pair,
    lse_pair,
    out_last,
    out_recv,
    lse_recv,
    part_send,
    part_recv,
    w_sem,
    wo_sem,
    cache_sem,
    q_send_sem,
    q_far_sem,
    q_near_sem,
    kv_send_sem,
    kv_recv_sem,
    x_send_sem,
    x_recv_sem,
    xl_send_sem,
    xl_recv_sem,
    o_send_sem,
    o_recv_sem,
    l_send_sem,
    l_recv_sem,
    p_send_sem,
    p_recv_sem,
):
    me = lax.axis_index("seq")
    head = lax.axis_index("head")
    rows, width = tokens_ref.shape
    requests = keys.shape[0]
    context = keys.shape[1]
    owners = TREE // rows
    q_width = wq_hbm.shape[1]
    groups = q_width // HEAD_WIDTH
    block = groups * rows
    queries = owners * block
    tiles = context // KEY_TILE
    own_request = me // owners
    own_place = me % owners
    scale = HEAD_WIDTH**-0.5
    scale2 = scale * math.log2(math.e)

    small = [
        pltpu.make_async_copy(source, target, small_sem.at[n])
        for n, (source, target) in enumerate(
            (
                (tokens_hbm, tokens_ref),
                (gain_hbm, gain_ref),
                (parents_hbm, parents_ref),
                (lengths_hbm, lengths_ref),
                (slots_hbm, slots_ref),
            )
        )
    ]
    for copy in small[:2]:
        copy.start()
    part = width // WEIGHT_PARTS

    wide = 2 * HEAD_WIDTH
    pieces = q_width // wide

    def start_weights(source, first, column, sem):
        for c in range(WEIGHT_PARTS):
            at = pl.ds(c * part, part)
            count = min(wide, source.shape[1])
            pltpu.make_async_copy(
                source.at[at, pl.ds(first, count)],
                wqkv.at[at, pl.ds(column, count)],
                w_sem.at[sem],
            ).start()

    def project(n):
        at = wqkv.at[:, pl.ds(n * wide, wide)]
        pltpu.make_async_copy(at, at, w_sem.at[n]).wait()
        return jnp.dot(
            normed[...],
            wqkv[:, n * wide : (n + 1) * wide],
            preferred_element_type=F32,
        ).astype(BF16)

    own_width = width // n_head

    def wo_copy(j):
        at = pl.ds(pl.multiple_of(j * own_width, own_width), own_width)
        return pltpu.make_async_copy(wo_hbm.at[:, at], wo.at[j], wo_sem)

    core = own_place % 2
    spot = own_place // 2
    chip = me // 2
    partner = me + 1 - 2 * core
    lanes = 128
    chips = n_seq // 2
    chips_x = 2
    joined = requests - 2
    unforwarded = 1

    rows_y = requests // chips_x

    def request_at(i):
        y = (own_request // chips_x + ORDER[i][0]) % rows_y
        return y * chips_x + (own_request + ORDER[i][1]) % chips_x

    def user_at(i):
        y = (own_request // chips_x + rows_y - ORDER[i][0]) % rows_y
        return y * chips_x + (own_request + ORDER[i][1]) % chips_x

    start_weights(wq_hbm, 0, 0, 0)

    barrier = pltpu.get_barrier_semaphore()

    def greet_seq(j, _):
        pl.semaphore_signal(
            barrier,
            inc=1,
            device_id=((me + j) % n_seq, head),
            device_id_type=pl.DeviceIdType.MESH,
        )
        return 0

    def greet_head(j, _):
        pl.semaphore_signal(
            barrier,
            inc=1,
            device_id=(me, (head + j) % n_head),
            device_id_type=pl.DeviceIdType.MESH,
        )
        return 0

    for n in sorted(range(1, n_head), key=lambda d: -min(d, n_head - d)):
        greet_head(n, 0)
    lax.fori_loop(1, n_seq, greet_seq, 0)

    for n in range(1, pieces):
        start_weights(wq_hbm, n * wide, n * wide, n)
    for copy in small[2:]:
        copy.start()

    def start_wo(j, _):
        wo_copy(j).start()
        return 0

    small[0].wait()
    small[1].wait()
    inputs = tokens_ref[...].astype(F32)
    mean = jnp.mean(inputs * inputs, axis=-1, keepdims=True)
    normed[...] = (
        inputs
        * lax.rsqrt(mean + NORM_EPSILON)
        * gain_ref[...].reshape(1, width).astype(F32)
    ).astype(BF16)

    for n in range(pieces):
        projected = project(n)
        if n == 0:
            start_weights(wk_hbm, 0, q_width, pieces)
            start_weights(wv_hbm, 0, q_width + HEAD_WIDTH, pieces)
        for g in range(2):
            line = (n * 2 + g) * rows
            qall[me, line : line + rows, :] = projected[
                :, g * HEAD_WIDTH : (g + 1) * HEAD_WIDTH
            ]

    def remote(source, target, send_sem, recv_sem, peer):
        return pltpu.make_async_remote_copy(
            src_ref=source,
            dst_ref=target,
            send_sem=send_sem,
            recv_sem=recv_sem,
            device_id=(peer, head),
            device_id_type=pl.DeviceIdType.MESH,
        )

    def arrived(ref, count, sem):
        at = pl.ds(0, count)
        pltpu.make_async_copy(ref.at[at], ref.at[at], sem).wait()

    def q_copy(which, recv_sem, peer):
        return remote(qall.at[which], qall.at[which], q_send_sem, recv_sem, peer)

    pl.semaphore_wait(barrier, n_seq - 1 + n_head - 1)

    def q_send(i):
        for n in range(2):
            to = user_at(i) * owners + (spot + n) % 2 * 2
            q_copy(me, q_far_sem.at[own_request], to + core).start()
            if i < unforwarded:
                q_copy(me, q_near_sem.at[own_request], to + 1 - core).start()

    q_send(0)
    q_send(1)
    for i in range(requests):
        r = request_at(i)
        for source, target in ((keys_hbm, keys), (values_hbm, values)):
            pltpu.make_async_copy(source.at[r], target.at[r], cache_sem.at[r]).start()
    lax.fori_loop(0, n_head, start_wo, 0)

    projected = project(pieces)
    for n in range(2):
        kvtree[own_place, n * rows : (n + 1) * rows, :] = projected[
            :, n * HEAD_WIDTH : (n + 1) * HEAD_WIDTH
        ]

    q_send(2)
    q_send(3)

    for copy in small[2:]:
        copy.wait()
    parent = parents_ref[pl.ds(own_request, 1), :]
    node = lax.broadcasted_iota(jnp.int32, (TREE, TREE), 0)
    other = lax.broadcasted_iota(jnp.int32, (TREE, TREE), 1)
    reached = jnp.where((parent == node) | (node == other), 1.0, 0.0)
    for _ in range(max(1, (TREE - 1).bit_length())):
        half = reached.astype(BF16)
        reached = jnp.minimum(jnp.dot(half, half, preferred_element_type=F32), 1.0)

    for n in range(1, owners):
        peer = own_request * owners + (own_place + n) % owners
        mine = kvtree.at[own_place]
        remote(mine, mine, kv_send_sem, kv_recv_sem, peer).start()
    q_send(4)
    q_send(5)

    row_in_page = lax.broadcasted_iota(jnp.int32, (PAGE, queries), 0)

    def forward(i):
        r = request_at(i)
        base = r * owners + core
        if i == requests - 1:
            arrived(qall, 1, q_far_sem.at[r])
            q_copy(beside, q_near_sem.at[r], partner).start()
        else:
            arrived(qall, 2, q_far_sem.at[r])
            q_copy(base, q_near_sem.at[r], partner).start()
            q_copy(base + 2, q_near_sem.at[r], partner).start()

    def wait_for(i):
        r = request_at(i)
        if i < unforwarded:
            arrived(qall, 2, q_far_sem.at[r])
        arrived(qall, 2, q_near_sem.at[r])
        arrived(keys, 2, cache_sem.at[r])

    def score_tile(i, b, best, score):
        r = request_at(i)
        q = qall[pl.ds(r * owners, owners)].reshape(queries, HEAD_WIDTH)
        s = lax.dot_general(
            keys[r, b * KEY_TILE : (b + 1) * KEY_TILE, :],
            q,
            NT,
            preferred_element_type=F32,
        )
        for n in range(KEY_TILE // PAGE):
            p = b * (KEY_TILE // PAGE) + n
            left = lengths_ref[r] - slots_ref[r, p] * PAGE
            shown = jnp.where(
                row_in_page < left, s[n * PAGE : (n + 1) * PAGE], HIDDEN
            )
            score[p * PAGE : (p + 1) * PAGE, :] = shown
            high = jnp.max(shown.reshape(PAGE // 8, 8, queries), axis=0)
            best = high if best is None else jnp.maximum(best, high)
        return best

    def weigh_tile(i, b, state, score, top):
        r = request_at(i)
        acc, total = state
        w = jnp.exp2(score[b * KEY_TILE : (b + 1) * KEY_TILE, :] * scale2 - top)
        low = jnp.sum(w.reshape(KEY_TILE // 8, 8, queries), axis=0)
        added = lax.dot_general(
            values[r, b * KEY_TILE : (b + 1) * KEY_TILE, :],
            w.astype(BF16),
            TN,
            preferred_element_type=F32,
        )
        if acc is None:
            return added, low
        return acc + added, total + low

    def finish(i, state, top, last):
        acc, total = state
        total = jnp.maximum(jnp.sum(total, axis=0, keepdims=True), 1.0)
        out = acc / total
        lse = top * (1.0 / math.log2(math.e)) + jnp.log(total)
        for n in range(2):
            half = slice(n * lanes, (n + 1) * lanes)
            lse_own[i, n] = lse[:, half]
            if not last:
                out_own[i, n] = out[:, half].astype(BF16)
        if last:
            out = out.T.astype(BF16).reshape(owners, block, HEAD_WIDTH)
            out_last[i - joined] = out

    def swap(i):
        other = 1 - core
        remote(
            out_own.at[i, other], out_swap.at[i], x_send_sem, x_recv_sem.at[i], partner
        ).start()
        remote(
            lse_own.at[i, other],
            lse_swap.at[i],
            xl_send_sem,
            xl_recv_sem.at[i],
            partner,
        ).start()

    def wait_swap(i):
        arrived(out_swap, 1, x_recv_sem.at[i])
        arrived(lse_swap, 1, xl_recv_sem.at[i])

    def join(i):
        mine, theirs = lse_own[i, core], lse_swap[i]
        high = jnp.maximum(mine, theirs)
        mine = jnp.exp(mine - high)
        theirs = jnp.exp(theirs - high)
        total = mine + theirs
        out = out_own[i, core].astype(F32) * (mine / total)
        out += out_swap[i].astype(F32) * (theirs / total)
        out_pair[i] = out.T.astype(BF16).reshape(2, block, HEAD_WIDTH)
        lse_pair[i] = high + jnp.log(total)

    def send_pair(i):
        first = request_at(i) * owners + core * 2

        for n in range(2):
            place = (core + n) % 2
            peer = first + place
            remote(
                out_pair.at[i, place], out_recv.at[chip], o_send_sem, o_recv_sem, peer
            ).start()
            remote(
                lse_pair.at[i], lse_recv.at[chip], l_send_sem, l_recv_sem, peer
            ).start()

    def send_direct(i):
        r = request_at(i)
        own = i == requests - 1
        spare = chips + (i - joined) * 2 + chip % 2
        slot = chip * (1 - core) + spare * core

        def send(n, _):
            place = (own_place + n) % owners
            peer = r * owners + place
            remote(
                out_last.at[i - joined, place],
                out_recv.at[slot],
                o_send_sem,
                o_recv_sem,
                peer,
            ).start()
            remote(
                lse_own.at[i, place // 2],
                lse_recv.at[slot],
                l_send_sem,
                l_recv_sem,
                peer,
            ).start()
            return 0

        lax.fori_loop(1 if own else 0, owners, send, 0)
        if own:
            out_recv[slot] = out_last[i - joined, own_place]
            lse_recv[slot] = lse_own[i, spot]

    def half_step(i, now, after):
        joins = i >= 2
        direct = i >= joined
        if i == 0:
            forward(1)
        if i + 2 < requests:
            forward(i + 2)
        if after is not None:
            wait_for(i + 1)
        if joins:
            wait_swap(i - 2)
        score, top_ref = now
        top = jnp.max(top_ref[...], axis=0, keepdims=True) * scale2
        state = (None, None)
        best = None
        for b in range(tiles):
            if after is not None:
                best = score_tile(i + 1, b, best, after[0])
            state = weigh_tile(i, b, state, score, top)
        if after is not None:
            after[1][...] = best
        finish(i, state, top, direct)
        if joins:
            join(i - 2)
        if direct:
            send_direct(i)
        else:
            swap(i)
        if joins:
            send_pair(i - 2)

    a, b = (score_a, top_a), (score_b, top_b)
    wait_for(0)
    best = None
    for t in range(tiles):
        best = score_tile(0, t, best, score_a)
    top_a[...] = best
    q_send(6)
    q_copy(me, q_near_sem.at[own_request], partner).start()
    beside = own_request * owners + (1 - spot) * 2 + core
    q_copy(me, q_far_sem.at[own_request], beside).start()
    for n in range(requests // 2):
        for i, now, after in ((2 * n, a, b), (2 * n + 1, b, a)):
            half_step(i, now, after if i < requests - 1 else None)

    arrived(kvtree, owners - 1, kv_recv_sem)
    own_queries = qall[me]
    own_queries = jnp.concatenate([own_queries] * (lanes // block), axis=0)
    tree_keys = kvtree[:, :rows, :].reshape(TREE, HEAD_WIDTH)
    tree_values = kvtree[:, rows:, :].reshape(TREE, HEAD_WIDTH)
    token = lax.broadcasted_iota(jnp.int32, (TREE, lanes), 0)
    lane = lax.broadcasted_iota(jnp.int32, (TREE, lanes), 1)
    pick = jnp.where(token == own_place * rows + lane % rows, 1.0, 0.0).astype(BF16)
    seen = jnp.dot(reached.astype(BF16), pick, preferred_element_type=F32) > 0.5
    tree_scores = lax.dot_general(
        tree_keys, own_queries, NT, preferred_element_type=F32
    )
    tree_scores = jnp.where(seen, tree_scores, HIDDEN)
    tree_top = jnp.max(tree_scores, axis=0, keepdims=True)
    tree_weights = jnp.where(
        seen, jnp.exp2(tree_scores * scale2 - tree_top * scale2), 0.0
    )
    tree_total = jnp.maximum(jnp.sum(tree_weights, axis=0, keepdims=True), 1.0)
    tree_sum = lax.dot_general(
        tree_values, tree_weights.astype(BF16), TN, preferred_element_type=F32
    )
    blocks = chips + 2 * (requests - joined)
    out_recv[blocks] = (tree_sum / tree_total).T[:block].astype(BF16)
    lse_recv[blocks] = tree_top * scale + jnp.log(tree_total)
    for n in range(blocks + 1, lse_recv.shape[0]):
        lse_recv[n] = jnp.full((1, lanes), HIDDEN, F32)
    arrived(wo, n_head, wo_sem)

    arrived(lse_recv, blocks - 1, l_recv_sem)
    lse = lse_recv[...].reshape(lse_recv.shape[0], lanes)
    lse = pltpu.roll(lse, (lanes - core * block) % lanes, 1)
    factor = jnp.exp(lse - jnp.max(lse, axis=0, keepdims=True))
    factor = (factor / jnp.sum(factor, axis=0, keepdims=True)).T[:block]
    arrived(out_recv, blocks - 1, o_recv_sem)
    merged = jnp.zeros((block, HEAD_WIDTH), F32)
    for n in range(blocks + 1):
        merged += out_recv[n].astype(F32) * factor[:, n : n + 1]
    merged = merged.astype(BF16)
    attended = jnp.concatenate(
        [merged[g * rows : (g + 1) * rows] for g in range(groups)], axis=1
    )

    def piece(j):
        return jnp.dot(attended, wo[j], preferred_element_type=F32)

    def part_copy(j):
        return pltpu.make_async_remote_copy(
            src_ref=part_send.at[j],
            dst_ref=part_recv.at[head],
            send_sem=p_send_sem,
            recv_sem=p_recv_sem,
            device_id=(me, j),
            device_id_type=pl.DeviceIdType.MESH,
        )

    order = sorted(range(1, n_head), key=lambda d: -min(d, n_head - d))
    for n, d in enumerate(order):
        j = (head + d) % n_head
        part_send[j] = piece(j).astype(BF16)
        if n > 0:
            part_copy((head + order[n - 1]) % n_head).start()
    mine = piece(head)
    part_copy((head + order[-1]) % n_head).start()
    at = pl.ds(pl.multiple_of(head * own_width, own_width), own_width)
    mine = mine + tokens_ref[:, at].astype(F32)
    part_recv[head] = jnp.zeros((rows, own_width), BF16)
    arrived(part_recv, n_head - 1, p_recv_sem)
    mixed_ref[...] = (mine + jnp.sum(part_recv[...].astype(F32), axis=0)).astype(BF16)

    arrived(part_send, n_head - 1, p_send_sem)
    arrived(qall, n_seq - 1, q_send_sem)
    arrived(kvtree, owners - 1, kv_send_sem)
    arrived(out_swap, joined, x_send_sem)
    arrived(lse_swap, joined, xl_send_sem)
    arrived(out_recv, blocks - 1, o_send_sem)
    arrived(lse_recv, blocks - 1, l_send_sem)


def per_device(
    tokens,
    norm_gain,
    w_query,
    key_projection,
    value_projection,
    w_out,
    cache_keys,
    paged_value_cache,
    lengths,
    parents,
    slot_block,
):
    n_seq = lax.axis_size("seq")
    n_head = lax.axis_size("head")
    rows, width = tokens.shape
    requests, context, _ = cache_keys.shape
    q_width = w_query.shape[1]
    groups = q_width // HEAD_WIDTH
    owners = TREE // rows
    block = groups * rows
    queries = owners * block
    own_width = width // n_head
    vmem = pl.BlockSpec(memory_space=pltpu.VMEM)
    hbm = pl.BlockSpec(memory_space=pltpu.HBM)
    dma = pltpu.SemaphoreType.DMA
    return pl.pallas_call(
        functools.partial(layer, n_seq, n_head),
        out_shape=pltpu.VMEM((rows, own_width), BF16),
        in_specs=[hbm] * 11,
        out_specs=vmem,
        scratch_shapes=[
            pltpu.SMEM(lengths.shape, jnp.int32),
            pltpu.SMEM(slot_block.shape, jnp.int32),
            pltpu.VMEM(tokens.shape, BF16),
            pltpu.VMEM(norm_gain.shape, BF16),
            pltpu.VMEM(parents.shape, jnp.int32),
            dma((5,)),
            pltpu.VMEM((width, q_width + 2 * HEAD_WIDTH), BF16),
            pltpu.VMEM((n_head, q_width, own_width), BF16),
            pltpu.VMEM((requests, context, HEAD_WIDTH), BF16),
            pltpu.VMEM((requests, context, HEAD_WIDTH), BF16),
            pltpu.VMEM((rows, width), BF16),
            pltpu.VMEM((n_seq, block, HEAD_WIDTH), BF16),
            pltpu.VMEM((owners, 2 * rows, HEAD_WIDTH), BF16),
            pltpu.VMEM((context, queries), F32),
            pltpu.VMEM((context, queries), F32),
            pltpu.VMEM((8, queries), F32),
            pltpu.VMEM((8, queries), F32),
            pltpu.VMEM((requests, 2, HEAD_WIDTH, 2 * block), BF16),
            pltpu.VMEM((requests, 2, 1, 2 * block), F32),
            pltpu.VMEM((requests, HEAD_WIDTH, 2 * block), BF16),
            pltpu.VMEM((requests, 1, 2 * block), F32),
            pltpu.VMEM((requests, 2, block, HEAD_WIDTH), BF16),
            pltpu.VMEM((requests, 1, 2 * block), F32),
            pltpu.VMEM((2, owners, block, HEAD_WIDTH), BF16),
            pltpu.VMEM((24, block, HEAD_WIDTH), BF16),
            pltpu.VMEM((24, 1, 2 * block), F32),
            pltpu.VMEM((n_head, rows, own_width), BF16),
            pltpu.VMEM((n_head, rows, own_width), BF16),
            dma((q_width // (2 * HEAD_WIDTH) + 1,)),
            dma,
            dma((requests,)),
            dma,
            dma((requests,)),
            dma((requests,)),
            dma,
            dma,
            dma,
            dma((requests - 2,)),
            dma,
            dma((requests - 2,)),
            dma,
            dma,
            dma,
            dma,
            dma,
            dma,
        ],
        compiler_params=pltpu.CompilerParams(
            collective_id=0,
            has_side_effects=True,
            vmem_limit_bytes=60 * 1024 * 1024,
        ),
        name="layer",
    )(
        lengths,
        slot_block,
        tokens,
        norm_gain,
        parents,
        w_query,
        key_projection,
        value_projection,
        w_out,
        cache_keys,
        paged_value_cache,
    )


def solution(mesh):
    in_specs = (
        P("seq", None),
        P(),
        P(None, "head"),
        P(None, "head"),
        P(None, "head"),
        P("head", None),
        P(None, "seq", "head"),
        P(None, "seq", "head"),
        P(),
        P(),
        P(None, "seq"),
    )
    return jax.shard_map(
        per_device,
        mesh=mesh,
        in_specs=in_specs,
        out_specs=P("seq", "head"),
        check_vma=False,
    )
```

time: 36.9 us -> 35.8 us (0.970)
  Pallas kernels: 36.2 us -> 35.1 us
    pallas_call x1, Pallas kernels: 36.2 us -> 35.1 us  [per_device(): pl.pallas_call(functools.partial(layer, n_seq, n_head), out_shape=pltpu.V...]
where the time goes in v3:
time: 35.8 us; the launch traced here: 35.7 us
  Pallas kernels  35.1 us (98%)
  local copies, waits for them, and re-layouts  0.61 us (2%)
    pallas_call x1, Pallas kernels, per_device(): pl.pallas_call(functools.partial(layer, n_seq, n_head), out_shape=pltpu.V...  35.1 us

profile of v3, /device:TPU:1, one launch (start us, length us, event | category | flops | bytes accessed | tf_op | source)
XLA Modules:
  0.0 35.7 jit_solution(12688875449956252280)
XLA Ops:
  0.0 35.1 %layer.1 = bf16[16,512]{1,0:T(8,128)(2,1)S(1)} custom-call(s32[8]{0:T(128)} %lengths_hbm.1, s32[8,16]{1,0:T(8,128)} %slots_hbm.1, bf16[16,4096]{1,0:T(8,128)(2,1)} %tokens_hbm.1, bf16[4096]{0:T(1024)(128)(2,1)} %gain_hbm.1, s32[8,64]{1,0:T(8,128)} %parents_hbm.1, bf16[4096,512]{1,0:T(8,128)(2,1)} %wq_hbm.1, bf16[4096,128]{1,0:T(8,128)(2,1)} %wk_hbm.1, ...), custom_call_target="tpu_custom_call" | custom-call | tf_op jit(solution)/shard_map/layer/pallas_call | solution.py:573
  35.1 0.6 %copy.13 = bf16[16,512]{1,0:T(8,128)(2,1)} copy(bf16[16,512]{1,0:T(8,128)(2,1)S(1)} %layer.1) | data formatting | bytes 32768

commit v4 on v3

--- a/solution.py
+++ b/solution.py
@@ -15,7 +15,8 @@
 PAGE = 128
 KEY_TILE = 256
 WEIGHT_PARTS = 4
-ORDER = ((0, 1), (1, 0), (2, 0), (2, 1), (3, 1), (1, 1), (3, 0), (0, 0))
+ORDER = ((0, 1), (3, 0), (2, 0), (2, 1), (3, 1), (1, 1), (1, 0), (0, 0))
+FORWARDS = ((2,), (3, 4), (5,), (6,), (7,), (), (), ())
 
 NT = (((1,), (1,)), ((), ()))
 TN = (((0,), (0,)), ((), ()))
@@ -158,12 +159,9 @@
     rows_y = requests // chips_x
 
     def request_at(i):
-        y = (own_request // chips_x + ORDER[i][0]) % rows_y
-        return y * chips_x + (own_request + ORDER[i][1]) % chips_x
-
-    def user_at(i):
-        y = (own_request // chips_x + rows_y - ORDER[i][0]) % rows_y
-        return y * chips_x + (own_request + ORDER[i][1]) % chips_x
+        y = own_request // chips_x
+        row = (y, y + 1 - 2 * (y % 2), (y + 2) % rows_y, rows_y - 1 - y)[ORDER[i][0]]
+        return row * chips_x + (own_request + ORDER[i][1]) % chips_x
 
     start_weights(wq_hbm, 0, 0, 0)
 
@@ -242,7 +240,7 @@
 
     def q_send(i):
         for n in range(2):
-            to = user_at(i) * owners + (spot + n) % 2 * 2
+            to = request_at(i) * owners + (spot + n) % 2 * 2
             q_copy(me, q_far_sem.at[own_request], to + core).start()
             if i < unforwarded:
                 q_copy(me, q_near_sem.at[own_request], to + 1 - core).start()
@@ -261,8 +259,8 @@
             :, n * HEAD_WIDTH : (n + 1) * HEAD_WIDTH
         ]
 
+    q_send(3)
     q_send(2)
-    q_send(3)
 
     for copy in small[2:]:
         copy.wait()
@@ -422,12 +420,10 @@
             lse_recv[slot] = lse_own[i, spot]
 
     def half_step(i, now, after):
-        joins = i >= 2
+        joins = 2 <= i < requests - 1
         direct = i >= joined
-        if i == 0:
-            forward(1)
-        if i + 2 < requests:
-            forward(i + 2)
+        for n in FORWARDS[i]:
+            forward(n)
         if after is not None:
             wait_for(i + 1)
         if joins:
@@ -451,9 +447,14 @@
             swap(i)
         if joins:
             send_pair(i - 2)
+        if i == joined:
+            wait_swap(i - 1)
+            join(i - 1)
+            send_pair(i - 1)
 
     a, b = (score_a, top_a), (score_b, top_b)
     wait_for(0)
+    forward(1)
     best = None
     for t in range(tiles):
         best = score_tile(0, t, best, score_a)
@@ -522,13 +523,11 @@
         )
 
     order = sorted(range(1, n_head), key=lambda d: -min(d, n_head - d))
-    for n, d in enumerate(order):
+    for d in order:
         j = (head + d) % n_head
         part_send[j] = piece(j).astype(BF16)
-        if n > 0:
-            part_copy((head + order[n - 1]) % n_head).start()
+        part_copy(j).start()
     mine = piece(head)
-    part_copy((head + order[-1]) % n_head).start()
     at = pl.ds(pl.multiple_of(head * own_width, own_width), own_width)
     mine = mine + tokens_ref[:, at].astype(F32)
     part_recv[head] = jnp.zeros((rows, own_width), BF16)

time: 35.8 us -> 35.3 us (0.986)
  Pallas kernels: 35.1 us -> 34.6 us
    pallas_call x1, Pallas kernels: 35.1 us -> 34.6 us  [per_device(): pl.pallas_call(functools.partial(layer, n_seq, n_head), out_shape=pltpu.V...]
where the time goes in v4:
time: 35.3 us; the launch traced here: 35.2 us
  Pallas kernels  34.6 us (98%)
  local copies, waits for them, and re-layouts  0.61 us (2%)
    pallas_call x1, Pallas kernels, per_device(): pl.pallas_call(functools.partial(layer, n_seq, n_head), out_shape=pltpu.V...  34.6 us

profile of v4, /device:TPU:1, one launch (start us, length us, event | category | flops | bytes accessed | tf_op | source)
XLA Modules:
  0.0 35.2 jit_solution(12679598336477644541)
XLA Ops:
  0.0 34.6 %layer.1 = bf16[16,512]{1,0:T(8,128)(2,1)S(1)} custom-call(s32[8]{0:T(128)} %lengths_hbm.1, s32[8,16]{1,0:T(8,128)} %slots_hbm.1, bf16[16,4096]{1,0:T(8,128)(2,1)} %tokens_hbm.1, bf16[4096]{0:T(1024)(128)(2,1)} %gain_hbm.1, s32[8,64]{1,0:T(8,128)} %parents_hbm.1, bf16[4096,512]{1,0:T(8,128)(2,1)} %wq_hbm.1, bf16[4096,128]{1,0:T(8,128)(2,1)} %wk_hbm.1, ...), custom_call_target="tpu_custom_call" | custom-call | tf_op jit(solution)/shard_map/layer/pallas_call | solution.py:572
  34.6 0.6 %copy.13 = bf16[16,512]{1,0:T(8,128)(2,1)} copy(bf16[16,512]{1,0:T(8,128)(2,1)S(1)} %layer.1) | data formatting | bytes 32768

commit v5 on v4

--- a/solution.py
+++ b/solution.py
@@ -14,6 +14,7 @@
 TREE = 64
 PAGE = 128
 KEY_TILE = 256
+SCORE_TILE = 512
 WEIGHT_PARTS = 4
 ORDER = ((0, 1), (3, 0), (2, 0), (2, 1), (3, 1), (1, 1), (1, 0), (0, 0))
 FORWARDS = ((2,), (3, 4), (5,), (6,), (7,), (), (), ())
@@ -97,6 +98,7 @@
     block = groups * rows
     queries = owners * block
     tiles = context // KEY_TILE
+    every = SCORE_TILE // KEY_TILE
     own_request = me // owners
     own_place = me % owners
     scale = HEAD_WIDTH**-0.5
@@ -303,13 +305,13 @@
         r = request_at(i)
         q = qall[pl.ds(r * owners, owners)].reshape(queries, HEAD_WIDTH)
         s = lax.dot_general(
-            keys[r, b * KEY_TILE : (b + 1) * KEY_TILE, :],
+            keys[r, b * SCORE_TILE : (b + 1) * SCORE_TILE, :],
             q,
             NT,
             preferred_element_type=F32,
         )
-        for n in range(KEY_TILE // PAGE):
-            p = b * (KEY_TILE // PAGE) + n
+        for n in range(SCORE_TILE // PAGE):
+            p = b * (SCORE_TILE // PAGE) + n
             left = lengths_ref[r] - slots_ref[r, p] * PAGE
             shown = jnp.where(
                 row_in_page < left, s[n * PAGE : (n + 1) * PAGE], HIDDEN
@@ -433,9 +435,9 @@
         state = (None, None)
         best = None
         for b in range(tiles):
-            if after is not None:
-                best = score_tile(i + 1, b, best, after[0])
             state = weigh_tile(i, b, state, score, top)
+            if after is not None and b % every == 0:
+                best = score_tile(i + 1, b // every, best, after[0])
         if after is not None:
             after[1][...] = best
         finish(i, state, top, direct)
@@ -456,7 +458,7 @@
     wait_for(0)
     forward(1)
     best = None
-    for t in range(tiles):
+    for t in range(tiles // every):
         best = score_tile(0, t, best, score_a)
     top_a[...] = best
     q_send(6)

time: 35.3 us -> 35.2 us (level)
  no operation moved by 1% of the time
where the time goes in v5:
time: 35.2 us; the launch traced here: 35.1 us
  Pallas kernels  34.5 us (98%)
  local copies, waits for them, and re-layouts  0.61 us (2%)
    pallas_call x1, Pallas kernels, per_device(): pl.pallas_call(functools.partial(layer, n_seq, n_head), out_shape=pltpu.V...  34.5 us

profile of v5, /device:TPU:1, one launch (start us, length us, event | category | flops | bytes accessed | tf_op | source)
XLA Modules:
  0.0 35.1 jit_solution(3471468076582061184)
XLA Ops:
  0.0 34.5 %layer.1 = bf16[16,512]{1,0:T(8,128)(2,1)S(1)} custom-call(s32[8]{0:T(128)} %lengths_hbm.1, s32[8,16]{1,0:T(8,128)} %slots_hbm.1, bf16[16,4096]{1,0:T(8,128)(2,1)} %tokens_hbm.1, bf16[4096]{0:T(1024)(128)(2,1)} %gain_hbm.1, s32[8,64]{1,0:T(8,128)} %parents_hbm.1, bf16[4096,512]{1,0:T(8,128)(2,1)} %wq_hbm.1, bf16[4096,128]{1,0:T(8,128)(2,1)} %wk_hbm.1, ...), custom_call_target="tpu_custom_call" | custom-call | tf_op jit(solution)/shard_map/layer/pallas_call | solution.py:574
  34.5 0.6 %copy.13 = bf16[16,512]{1,0:T(8,128)(2,1)} copy(bf16[16,512]{1,0:T(8,128)(2,1)S(1)} %layer.1) | data formatting | bytes 32768

commit v6 on v5

--- a/solution.py
+++ b/solution.py
@@ -123,6 +123,9 @@
     wide = 2 * HEAD_WIDTH
     pieces = q_width // wide
 
+    halves = 2
+    deep = width // halves
+
     def start_weights(source, first, column, sem):
         for c in range(WEIGHT_PARTS):
             at = pl.ds(c * part, part)
@@ -130,17 +133,21 @@
             pltpu.make_async_copy(
                 source.at[at, pl.ds(first, count)],
                 wqkv.at[at, pl.ds(column, count)],
-                w_sem.at[sem],
+                w_sem.at[sem, c * halves // WEIGHT_PARTS],
             ).start()
 
     def project(n):
-        at = wqkv.at[:, pl.ds(n * wide, wide)]
-        pltpu.make_async_copy(at, at, w_sem.at[n]).wait()
-        return jnp.dot(
-            normed[...],
-            wqkv[:, n * wide : (n + 1) * wide],
-            preferred_element_type=F32,
-        ).astype(BF16)
+        total = None
+        for h in range(halves):
+            at = wqkv.at[pl.ds(h * deep, deep), pl.ds(n * wide, wide)]
+            pltpu.make_async_copy(at, at, w_sem.at[n, h]).wait()
+            added = jnp.dot(
+                normed[:, h * deep : (h + 1) * deep],
+                wqkv[h * deep : (h + 1) * deep, n * wide : (n + 1) * wide],
+                preferred_element_type=F32,
+            )
+            total = added if total is None else total + added
+        return total.astype(BF16)
 
     own_width = width // n_head
 
@@ -605,7 +612,7 @@
             pltpu.VMEM((24, 1, 2 * block), F32),
             pltpu.VMEM((n_head, rows, own_width), BF16),
             pltpu.VMEM((n_head, rows, own_width), BF16),
-            dma((q_width // (2 * HEAD_WIDTH) + 1,)),
+            dma((q_width // (2 * HEAD_WIDTH) + 1, 2)),
             dma,
             dma((requests,)),
             dma,

time: 35.2 us -> 35.2 us (level)
  no operation moved by 1% of the time
where the time goes in v6:
time: 35.2 us; the launch traced here: 35.1 us
  Pallas kernels  34.5 us (98%)
  local copies, waits for them, and re-layouts  0.61 us (2%)
    pallas_call x1, Pallas kernels, per_device(): pl.pallas_call(functools.partial(layer, n_seq, n_head), out_shape=pltpu.V...  34.5 us

profile of v6, /device:TPU:1, one launch (start us, length us, event | category | flops | bytes accessed | tf_op | source)
XLA Modules:
  0.0 35.1 jit_solution(18106891284371746632)
XLA Ops:
  0.0 34.5 %layer.1 = bf16[16,512]{1,0:T(8,128)(2,1)S(1)} custom-call(s32[8]{0:T(128)} %lengths_hbm.1, s32[8,16]{1,0:T(8,128)} %slots_hbm.1, bf16[16,4096]{1,0:T(8,128)(2,1)} %tokens_hbm.1, bf16[4096]{0:T(1024)(128)(2,1)} %gain_hbm.1, s32[8,64]{1,0:T(8,128)} %parents_hbm.1, bf16[4096,512]{1,0:T(8,128)(2,1)} %wq_hbm.1, bf16[4096,128]{1,0:T(8,128)(2,1)} %wk_hbm.1, ...), custom_call_target="tpu_custom_call" | custom-call | tf_op jit(solution)/shard_map/layer/pallas_call | solution.py:581
  34.5 0.6 %copy.13 = bf16[16,512]{1,0:T(8,128)(2,1)} copy(bf16[16,512]{1,0:T(8,128)(2,1)S(1)} %layer.1) | data formatting | bytes 32768

commit v7 on v6

--- a/solution.py
+++ b/solution.py
@@ -14,7 +14,7 @@
 TREE = 64
 PAGE = 128
 KEY_TILE = 256
-SCORE_TILE = 512
+SCORE_TILE = 256
 WEIGHT_PARTS = 4
 ORDER = ((0, 1), (3, 0), (2, 0), (2, 1), (3, 1), (1, 1), (1, 0), (0, 0))
 FORWARDS = ((2,), (3, 4), (5,), (6,), (7,), (), (), ())

time: 35.2 us -> 35.1 us (level)
  no operation moved by 1% of the time
where the time goes in v7:
time: 35.1 us; the launch traced here: 35 us
  Pallas kernels  34.4 us (98%)
  local copies, waits for them, and re-layouts  0.61 us (2%)
    pallas_call x1, Pallas kernels, per_device(): pl.pallas_call(functools.partial(layer, n_seq, n_head), out_shape=pltpu.V...  34.4 us

profile of v7, /device:TPU:1, one launch (start us, length us, event | category | flops | bytes accessed | tf_op | source)
XLA Modules:
  0.0 35.0 jit_solution(4186130678111858884)
XLA Ops:
  0.0 34.4 %layer.1 = bf16[16,512]{1,0:T(8,128)(2,1)S(1)} custom-call(s32[8]{0:T(128)} %lengths_hbm.1, s32[8,16]{1,0:T(8,128)} %slots_hbm.1, bf16[16,4096]{1,0:T(8,128)(2,1)} %tokens_hbm.1, bf16[4096]{0:T(1024)(128)(2,1)} %gain_hbm.1, s32[8,64]{1,0:T(8,128)} %parents_hbm.1, bf16[4096,512]{1,0:T(8,128)(2,1)} %wq_hbm.1, bf16[4096,128]{1,0:T(8,128)(2,1)} %wk_hbm.1, ...), custom_call_target="tpu_custom_call" | custom-call | tf_op jit(solution)/shard_map/layer/pallas_call | solution.py:581
  34.4 0.6 %copy.13 = bf16[16,512]{1,0:T(8,128)(2,1)} copy(bf16[16,512]{1,0:T(8,128)(2,1)S(1)} %layer.1) | data formatting | bytes 32768
